TPU v7x, 32 devices: a whole 2x2x4 slice. The times are simulated.
32 devices in a mesh: shift: 8 (over y, x, core), dom: 4 (over z).
Axes of the slice: x: 2, y: 2, z: 4, core: 2. Of those that a mesh axis runs over, the one named last changes fastest.
Arguments:
- samples: float32 [32, 64, 1024], P('dom'), may hold values from -6 to 6
- potential: float32 [32, 1024], P('dom'), may hold values from 0 to 4
Outputs:
- subspace: float32 [32, 64, 1024], P('dom')
- reduced_h: float32 [64, 64], replicated
- reduced_b: float32 [64, 64], replicated
All inputs are finite; a program needn't handle non-finite values.
Results may differ from a plain program's by a relative error of at most 0.00027.
Values sent between devices are 32-bit elements; how exact they have to be, the bound alone decides.
A program may use at most 128 MiB of HBM per device.

v0:
```python
import jax
import jax.numpy as jnp
from jax import lax
from jax.sharding import PartitionSpec as P

NX = 32
NY = 32


CENTRE = 3.0
RADIUS = 2.0
RIDGE = 0.01


def extended_2(x, sides, width):
    for axis, dim in sides:
        count, length = (lax.axis_size(axis), x.shape[dim])
        up = [(i, (i + 1) % count) for i in range(count - 1)]
        down = [(j, i) for i, j in up]
        last = lax.slice_in_dim(x, length - width, length, axis=dim)
        first = lax.slice_in_dim(x, 0, width, axis=dim)
        before = lax.ppermute(last, axis, up)
        after = lax.ppermute(first, axis, down)
        x = jnp.concatenate([before, x, after], axis=dim)
    return x


def plane_sum(values):
    extent = values.shape[-1]
    leading = [(0, 0)] * (values.ndim - 1)
    padded = jnp.pad(values, leading + [(NY, NY)])
    column = lax.broadcasted_iota(jnp.int32, (extent,), 0) % NY
    lower_ok = (column != 0).astype(values.dtype)
    upper_ok = (column != NY - 1).astype(values.dtype)
    return (
        padded[..., 0:extent]
        + padded[..., 2 * NY : 2 * NY + extent]
        + padded[..., NY - 1 : NY - 1 + extent] * lower_ok
        + padded[..., NY + 1 : NY + 1 + extent] * upper_ok
    )


def colsum(values):
    return jnp.sum(values, axis=(0, 2))


def on_device(samples, potential):
    nodes = lax.axis_size("shift")
    planes = samples.shape[0]
    order = lax.axis_index("shift").astype(jnp.float32)
    angle = jnp.pi * (order + 0.5) / nodes
    shift_re = CENTRE + RADIUS * jnp.cos(angle)
    shift_im = RADIUS * jnp.sin(angle)
    weight_re = RADIUS * jnp.cos(angle) / nodes
    weight_im = RADIUS * jnp.sin(angle) / nodes

    def inverses(onsite_part):
        diag_re = shift_re - onsite_part
        modulus = diag_re * diag_re + shift_im * shift_im
        return (diag_re / modulus, -shift_im / modulus)

    def apply_inv(vector, inv_pair):
        return jnp.stack(
            [
                vector[0] * inv_pair[0] - vector[1] * inv_pair[1],
                vector[0] * inv_pair[1] + vector[1] * inv_pair[0],
            ]
        )

    def combine(vector, hamil):
        return jnp.stack(
            [
                shift_re * vector[0] - shift_im * vector[1] - hamil[0],
                shift_re * vector[1] + shift_im * vector[0] - hamil[1],
            ]
        )

    onsite = (6.0 + potential)[:, None, :]
    inv_own = inverses(onsite)

    def shrink_operate(vector, onsite_inner):
        inner = vector[:, 1:-1]
        beside = vector[:, 2:] + vector[:, :-2] + plane_sum(inner)
        return combine(inner, onsite_inner * inner - beside)

    joined = jnp.concatenate([samples, potential[:, None, :]], axis=1)
    extended = extended_2(joined, (("dom", 0),), 2)
    ext_samples = extended[:, :-1]
    ext_onsite = 6.0 + extended[:, -1:]
    inv_ext = inverses(ext_onsite)
    first_ext = apply_inv(jnp.stack([ext_samples, jnp.zeros_like(ext_samples)]), inv_ext)
    image_ext = shrink_operate(first_ext, ext_onsite[1:-1])
    total_planes = planes * lax.axis_size("dom")
    plane_index = (
        lax.axis_index("dom") * planes - 1 + lax.broadcasted_iota(jnp.int32, (planes + 2,), 0)
    )
    inside = ((plane_index >= 0) & (plane_index < total_planes)).astype(jnp.float32)
    image_ext = image_ext * inside[None, :, None, None]
    image_one = image_ext[:, 1:-1]
    first_block_real = image_one[0]
    first_block_imag = image_one[1]
    first_set = jnp.stack(
        [
            colsum(first_block_real * first_block_real + first_block_imag * first_block_imag),
            colsum(first_block_real * samples),
            colsum(-first_block_imag * samples),
        ]
    )
    first_tot = lax.psum(first_set, "dom")
    inv_mid = (inv_ext[0][1:-1], inv_ext[1][1:-1])
    image_two = shrink_operate(apply_inv(image_ext, inv_mid), ext_onsite[2:-2])
    two_re = image_two[0]
    two_im = image_two[1]
    second_set = jnp.stack(
        [
            colsum(first_block_real * two_re + first_block_imag * two_im),
            colsum(first_block_real * two_im - first_block_imag * two_re),
            colsum(two_re * two_re + two_im * two_im),
            colsum(two_re * samples),
            colsum(-two_im * samples),
        ]
    )
    second_tot = lax.psum(second_set, "dom")
    totals = jnp.concatenate([first_tot, second_tot], axis=0)
    g_one = totals[0]
    q_one_re = totals[1]
    q_one_im = totals[2]
    g_mix_re = totals[3]
    g_mix_im = totals[4]
    g_two = totals[5]
    q_two_re = totals[6]
    q_two_im = totals[7]
    ridge = RIDGE * (g_one + g_two) / 2.0
    determ = (g_one + ridge) * (g_two + ridge) - (g_mix_re * g_mix_re + g_mix_im * g_mix_im)
    coef_one_re = (
        (g_two + ridge) * q_one_re - (g_mix_re * q_two_re - g_mix_im * q_two_im)
    ) / determ
    coef_one_im = (
        (g_two + ridge) * q_one_im - (g_mix_re * q_two_im + g_mix_im * q_two_re)
    ) / determ
    coef_two_re = (
        (g_one + ridge) * q_two_re - (g_mix_re * q_one_re + g_mix_im * q_one_im)
    ) / determ
    coefficient_second_imag = (
        (g_one + ridge) * q_two_im - (g_mix_re * q_one_im - g_mix_im * q_one_re)
    ) / determ
    first_coefficient_real = coef_one_re[None, :, None]
    first_coefficient_imag = coef_one_im[None, :, None]
    second_coefficient_real = coef_two_re[None, :, None]
    second_coefficient_imag = coefficient_second_imag[None, :, None]
    solution = apply_inv(
        jnp.stack(
            [
                first_coefficient_real * samples
                + second_coefficient_real * first_block_real
                - second_coefficient_imag * first_block_imag,
                first_coefficient_imag * samples
                + second_coefficient_real * first_block_imag
                + second_coefficient_imag * first_block_real,
            ]
        ),
        inv_own,
    )
    weighted = weight_re * solution[0] - weight_im * solution[1]
    scale = 1.0 / (NX * NY * planes * lax.axis_size("dom"))
    subspace = lax.psum(weighted, "shift")
    padded = extended_2(subspace, (("dom", 0),), 1)
    applied = onsite * subspace - (padded[2:] + padded[:-2] + plane_sum(subspace))
    part_h = jnp.einsum("znc,zmc->nm", subspace, applied, precision=lax.Precision.HIGHEST) * scale
    part_b = jnp.einsum("znc,zmc->nm", subspace, subspace, precision=lax.Precision.HIGHEST) * scale
    reduced_h, reduced_b = lax.psum((part_h, part_b), "dom")
    return (subspace, reduced_h, reduced_b)


def solution(mesh):
    in_specs = (P("dom", None, None), P("dom", None))
    out_specs = (P("dom", None, None), P(), P())
    return jax.shard_map(
        on_device, mesh=mesh, in_specs=in_specs, out_specs=out_specs, check_vma=False
    )
```

profile of v0, /device:TPU:0, one launch (start us, length us, event | category | flops | bytes accessed | tf_op | source)
XLA Modules:
  0.0 185.9 jit_solution(1204473247824905076)
XLA Ops:
  7.2 1.7 constant_dynamic-update-slice_fusion
  9.2 0.4 copy.8
  9.7 5.0 %collective-permute-start = (f32[2,65,1024]{2,0,1:T(2,128)S(1)}, f32[2,65,1024]{2,0,1:T(2,128)S(1)}, u32[]{:S(2)}, u32[]{:S(2)}) collective-permute-start(f32[2,65,1024]{2,0,1:T(2,128)S(1)} %copy.8), channel_id=1, source_target_pairs={{0,1},{1,2},{2,3},{4,5},{5,6},{6,7},{8,9},{9,10},{10,11},{12,13},{... | collective-permute-start | bytes 1597448 | tf_op jit(solution)/shard_map/ppermute | solution.py:22
  14.7 1.2 copy.9
  15.9 1.3 collective-permute-start.1
  17.3 0.6 broadcast_add_fusion
  18.0 8.0 %collective-permute-done = f32[2,65,1024]{2,0,1:T(2,128)S(1)} collective-permute-done((f32[2,65,1024]{2,0,1:T(2,128)S(1)}, f32[2,65,1024]{2,0,1:T(2,128)S(1)}, u32[]{:S(2)}, u32[]{:S(2)}) %collective-permute-start) | collective-permute-done | bytes 532512 | tf_op jit(solution)/shard_map/ppermute | solution.py:22
  26.0 0.2 copy.10
  26.1 5.5 %collective-permute-done.1 = f32[2,65,1024]{2,0,1:T(2,128)} collective-permute-done((f32[2,65,1024]{2,0,1:T(2,128)}, f32[2,65,1024]{2,0,1:T(2,128)}, u32[]{:S(2)}, u32[]{:S(2)}) %collective-permute-start.1) | collective-permute-done | bytes 532512 | tf_op jit(solution)/shard_map/ppermute | solution.py:23
  31.6 1.2 copy.11
  33.1 0.3 pad_maximum_fusion.2
  33.4 0.2 copy-done.3
  33.7 0.9 add_bitcast_fusion
  34.6 2.8 %fusion.9 = f32[2,10,64,1024]{3,2,1,0:T(8,128)} fusion(f32[1,12,64,1024]{3,2,1,0:T(8,128)S(1)} %get-tuple-element.29, f32[1,12,64,1024]{3,2,1,0:T(8,128)S(1)} %get-tuple-element.28), kind=kLoop, calls=%fused_computation.21 | loop fusion | flops 1310720 | bytes 11534336 | tf_op jit(solution)/shard_map/stack | solution.py:63
  37.4 13.4 %fusion.4 = f32[2,10,64,1024]{3,2,1,0:T(8,128)} fusion(f32[2,10,64,1024]{3,2,1,0:T(8,128)} %fusion.9, f32[1,12,64,1024]{3,2,1,0:T(8,128)S(1)} %get-tuple-element.29, f32[1,12,64,1024]{3,2,1,0:T(8,128)S(1)} %get-tuple-element.28, f32[1024]{0:T(1024)S(1)} %get-tuple-element.45, f32[1024]{0:T(1024)S(1)} %get-tuple-element.44, f32[10,1024]{1,0:T(8,128)S(1)} %bitcast.188), kind=kLoop, calls=%fused_computation.16 | loop fusion | flops 14417920 | bytes 16826368 | tf_op jit(solution)/shard_map/sub | solution.py:84
  50.8 3.8 %slice_subtract_fusion.1 = (f32[1,10,64,1024]{3,2,1,0:T(8,128)S(1)}, f32[1,10,64,1024]{3,2,1,0:T(8,128)S(1)}) fusion(f32[2,10,64,1024]{3,2,1,0:T(8,128)} %fusion.4, f32[1,12,64,1024]{3,2,1,0:T(8,128)S(1)} %get-tuple-element.28, f32[1,12,64,1024]{3,2,1,0:T(8,128)S(1)} %get-tuple-element.29, f32[]{:T(128)S(6)} %mul.491, f32[]{:T(128)S(6)} %add_shard_map.3), kind=kLoop, calls=%fused_computation.43 | loop fusion | flops 5242880 | bytes 15728648 | tf_op jit(solution)/shard_map/sub | solution.py:73
  54.7 0.9 maximum_multiply_fusion
  55.6 1.3 multiply_add_fusion
  56.8 0.6 fusion.19
  57.4 4.8 %fusion.14 = f32[2,8,64,1024]{3,2,1,0:T(8,128)S(1)} fusion(f32[2,8,64,1024]{3,2,1,0:T(8,128)S(1)} %fusion.19, f32[1,10,64,1024]{3,2,1,0:T(8,128)S(1)} %get-tuple-element.27, f32[1,10,64,1024]{3,2,1,0:T(8,128)S(1)} %get-tuple-element.26, f32[1024]{0:T(1024)S(1)} %get-tuple-element.45, f32[1024]{0:T(1024)S(1)} %get-tuple-element.44, f32[8,1024]{1,0:T(8,128)S(1)} %bitcast.189), kind=kLoop, calls=%fused_computation.32 | loop fusion | flops 11534336 | bytes 13672448 | tf_op jit(solution)/shard_map/sub | solution.py:84
  62.3 1.5 fusion.36
  63.9 2.0 %multiply_reduce_fusion.1 = (f32[64]{0:T(128)S(1)}, f32[64]{0:T(128)S(1)}, f32[64]{0:T(128)S(1)}, f32[64]{0:T(128)S(1)}, f32[64]{0:T(128)S(1)}, /*index=5*/f32[64]{0:T(128)S(1)}, f32[64]{0:T(128)S(1)}, f32[64]{0:T(128)S(1)}) fusion(f32[8,64,1024]{2,1,0:T(8,128)S(1)} %copy-done.2, f32[2,10,64,1024]{3,2,1,0:T(8,128)S(1)} %maximum_multiply_fusion, ...), kind=kLoop, calls=%fused_computation.72 | loop fusion | flops 13630976 | bytes 10487808 | tf_op jit(solution)/shard_map/reduce_sum | solution.py:44
  66.0 10.3 %all-reduce.4 = (f32[5,64]{1,0:T(8,128)S(1)}, f32[3,64]{1,0:T(4,128)S(1)}) all-reduce(f32[5,64]{1,0:T(8,128)S(1)} %stack.59, f32[3,64]{1,0:T(4,128)S(1)} %pad_maximum_fusion.6), channel_id=1, replica_groups=mesh['shift'=8,'dom'=4] {'dom'}, use_global_device_ids=true, to_apply=%region_5.6 | all-reduce | flops 512 | bytes 4096 | tf_op jit(solution)/shard_map/psum | solution.py:123
  76.3 4.9 %multiply_subtract_fusion.1 = f32[8,64,1024]{2,1,0:T(8,128)} fusion(f32[8,64,1024]{2,1,0:T(8,128)S(1)} %copy-done.2, f32[2,10,64,1024]{3,2,1,0:T(8,128)} %copy-done, f32[]{:T(128)S(6)} %div.77, f32[8,1024]{1,0:T(8,128)S(1)} %get-tuple-element.38, f32[64]{0:T(128)S(1)} %fusion.65, f32[8,1024]{1,0:T(8,128)S(1)} %get-tuple-element.39, ...), kind=kLoop, calls=%fused_computation.70 | loop fusion | flops 9961472 | bytes 8455176 | tf_op jit(solution)/shard_map/sub | solution.py:164
  81.3 60.2 %all-reduce.7.cloned.1.call-done = f32[8,64,1024]{2,1,0:T(8,128)} async-done(((f32[8,64,1024]{2,1,0:T(8,128)}), f32[8,64,1024]{2,1,0:T(8,128)}) %all-reduce.7.cloned.1.call-update) | async-done | bytes 2097168 | tf_op jit(solution)/shard_map/psum | solution.py:166
  141.5 1.2 fusion.78
  142.7 1.3 collective-permute-start.2
  144.0 4.6 %collective-permute-start.3 = (f32[1,64,1024]{2,1,0:T(8,128)S(1)}, f32[1,64,1024]{2,1,0:T(8,128)S(1)}, u32[]{:S(2)}, u32[]{:S(2)}) collective-permute-start(f32[1,64,1024]{2,1,0:T(8,128)S(1)} %get-tuple-element.33), channel_id=1, source_target_pairs={{0,1},{1,2},{2,3},{4,5},{5,6},{6,7},{8,9},{9,10},{10,11},{12,13},{... | collective-permute-start | bytes 786440 | tf_op jit(solution)/shard_map/ppermute | solution.py:22
  148.6 4.0 %fusion.41 = f32[64,64]{1,0:T(8,128)S(1)} fusion(f32[8,64,1024]{2,1,0:T(8,128)} %all-reduce.7.cloned.1.call-done), kind=kOutput, calls=%fused_computation.81 | convolution fusion | flops 402657280 | bytes 2113536 | tf_op jit(solution)/shard_map/znc,zmc->nm/dot_general | solution.py:170
  152.7 3.8 %fusion.42 = f32[64,64]{1,0:T(8,128)S(1)} fusion(f32[8,64,1024]{2,1,0:T(8,128)S(1)} %copy-done.1, f32[1,64,1024]{2,1,0:T(8,128)S(1)} %collective-permute-done.3, f32[1,64,1024]{2,1,0:T(8,128)S(1)} %collective-permute-done.2, f32[1024]{0:T(1024)S(1)} %get-tuple-element.45, f32[1024]{0:T(1024)S(1)} %get-tuple-element.44, f32[8,1024]{1,0:T(8,128)S(1)} %copy-done.5), kind=kOutput, calls=%fused_computation.82 | convolution fusion | flops 408424448 | bytes 4775936 | tf_op jit(solution)/shard_map/znc,zmc->nm/dot_general | solution.py:169
  156.5 21.2 %all-reduce.3 = (f32[64,64]{1,0:T(8,128)}, f32[64,64]{1,0:T(8,128)}) all-reduce(f32[64,64]{1,0:T(8,128)S(1)} %fusion.42, f32[64,64]{1,0:T(8,128)S(1)} %fusion.41), channel_id=1, replica_groups=mesh['shift'=8,'dom'=4] {'dom'}, use_global_device_ids=true, to_apply=%region_11.12 | all-reduce | flops 8192 | bytes 65536 | tf_op jit(solution)/shard_map/psum | solution.py:171
  177.7 1.3 copy.40
  (37 shorter events, 0.8 us)
Async XLA Ops:
  7.2 1.8 copy-start.4
  7.2 134.3 %all-reduce.7.cloned.1.call-start = ((), (), s32[]{:S(2)}) async-start(), calls=%async_computation | async-start | bytes 4194304 | tf_op jit(solution)/shard_map/psum | solution.py:166
  9.7 16.3 %collective-permute-start = (f32[2,65,1024]{2,0,1:T(2,128)S(1)}, f32[2,65,1024]{2,0,1:T(2,128)S(1)}, u32[]{:S(2)}, u32[]{:S(2)}) collective-permute-start(f32[2,65,1024]{2,0,1:T(2,128)S(1)} %copy.8), channel_id=1, source_target_pairs={{0,1},{1,2},{2,3},{4,5},{5,6},{6,7},{8,9},{9,10},{10,11},{12,13},{... | collective-permute-start | bytes 1597448 | tf_op jit(solution)/shard_map/ppermute | solution.py:22
  15.9 15.8 %collective-permute-start.1 = (f32[2,65,1024]{2,0,1:T(2,128)}, f32[2,65,1024]{2,0,1:T(2,128)}, u32[]{:S(2)}, u32[]{:S(2)}) collective-permute-start(f32[2,65,1024]{2,0,1:T(2,128)} %copy.9), channel_id=1, source_target_pairs={{1,0},{2,1},{3,2},{5,4},{6,5},{7,6},{9,8},{10,9},{11,10},{13,12},{... | collective-permute-start | bytes 1597448 | tf_op jit(solution)/shard_map/ppermute | solution.py:23
  33.0 0.7 copy-start.3
  50.8 3.9 %slice-start = ((f32[12,1,1024]{2,1,0:T(1,128)}), f32[10,1,1024]{2,1,0:T(1,128)S(1)}, s32[]{:S(2)}) async-start(f32[12,1,1024]{2,1,0:T(1,128)} %copy-done.3), calls=%async_computation.1 | async-start | bytes 81920 | tf_op jit(solution)/shard_map/slice | solution.py:110
  55.6 8.2 %copy-start = (f32[2,10,64,1024]{3,2,1,0:T(8,128)}, f32[2,10,64,1024]{3,2,1,0:T(8,128)S(1)}, u32[]{:S(2)}) copy-start(f32[2,10,64,1024]{3,2,1,0:T(8,128)S(1)} %maximum_multiply_fusion) | copy-start | bytes 15728644
  62.3 1.6 copy-start.2
  81.2 71.4 %copy-start.5 = (f32[8,1024]{1,0:T(8,128)S(1)}, f32[8,1024]{1,0:T(8,128)}, u32[]{:S(2)}) copy-start(f32[8,1024]{1,0:T(8,128)} %get-tuple-element.37) | copy-start | bytes 98308
  141.5 11.2 %copy-start.1 = (f32[8,64,1024]{2,1,0:T(8,128)S(1)}, f32[8,64,1024]{2,1,0:T(8,128)}, u32[]{:S(2)}) copy-start(f32[8,64,1024]{2,1,0:T(8,128)} %all-reduce.7.cloned.1.call-done) | copy-start | bytes 6291460
  142.7 9.9 %collective-permute-start.2 = (f32[1,64,1024]{2,1,0:T(8,128)S(1)}, f32[1,64,1024]{2,1,0:T(8,128)S(1)}, u32[]{:S(2)}, u32[]{:S(2)}) collective-permute-start(f32[1,64,1024]{2,1,0:T(8,128)S(1)} %get-tuple-element.32), channel_id=1, source_target_pairs={{1,0},{2,1},{3,2},{5,4},{6,5},{7,6},{9,8},{10,9},{11,10},{13,12},{... | collective-permute-start | bytes 786440 | tf_op jit(solution)/shard_map/ppermute | solution.py:23
  144.0 8.7 %collective-permute-start.3 = (f32[1,64,1024]{2,1,0:T(8,128)S(1)}, f32[1,64,1024]{2,1,0:T(8,128)S(1)}, u32[]{:S(2)}, u32[]{:S(2)}) collective-permute-start(f32[1,64,1024]{2,1,0:T(8,128)S(1)} %get-tuple-element.33), channel_id=1, source_target_pairs={{0,1},{1,2},{2,3},{4,5},{5,6},{6,7},{8,9},{9,10},{10,11},{12,13},{... | collective-permute-start | bytes 786440 | tf_op jit(solution)/shard_map/ppermute | solution.py:22
Sparse Core Ops, SparseCore 0:
  81.4 60.0 all-reduce.6
where the time goes:
time: 186 us
  waiting for transfers between devices  73.8 us (40%)
  other arithmetic  38.1 us (20%)
  blocking collectives  31.5 us (17%)
  between operations  14.5 us (8%)
  starting transfers between devices  12.2 us (7%)
  local copies, waits for them, and re-layouts  7.97 us (4%)
  matrix products  7.85 us (4%)
    psum x1, waiting for transfers between devices, on_device(): subspace = lax.psum(weighted, 'shift')  60.2 us
    psum x1, blocking collectives, on_device(): reduced_h, reduced_b = lax.psum((part_h, part_b), 'dom')  21.2 us
    sub x2, other arithmetic, shrink_operate(): return combine(inner, onsite_inner * inner - beside)  18.2 us
    psum x1, blocking collectives, on_device(): second_tot = lax.psum(second_set, 'dom')  10.3 us
    ppermute x2, starting transfers between devices, extended_2(): before = lax.ppermute(last, axis, up)  9.55 us
    ppermute x2, waiting for transfers between devices, extended_2(): before = lax.ppermute(last, axis, up)  8.03 us
    ppermute x2, waiting for transfers between devices, extended_2(): after = lax.ppermute(first, axis, down)  5.49 us
    sub x2, other arithmetic, combine(): shift_re * vector[0] - shift_im * vector[1] - hamil[0]  5.3 us
  transfers between devices with their start and end apart: 5, of which 3 were waited for; matrix products, arithmetic and copies ran while one was open for 3% of the time, Pallas kernels for 0%

commit v1 on v0

v1 whole, which is shorter than its diff:
```python
import functools
import math

import jax
import jax.numpy as jnp
from jax import lax
from jax.experimental import pallas as pl
from jax.experimental.pallas import tpu as pltpu
from jax.sharding import PartitionSpec as P

NX = 32
NY = 32
LANES = 128

CENTRE = 3.0
RADIUS = 2.0
RIDGE = 0.01
MESH = pl.DeviceIdType.MESH


def tiles_of(value):
    return [value[:, at : at + LANES] for at in range(0, value.shape[1], LANES)]


def plane_sum(value):
    tiles = tiles_of(value)
    lane = lax.broadcasted_iota(jnp.int32, tiles[0].shape, 1)
    column = lane % NY
    zero = jnp.zeros_like(tiles[0])
    out = []
    for at, tile in enumerate(tiles):
        before = tiles[at - 1] if at > 0 else zero
        after = tiles[at + 1] if at + 1 < len(tiles) else zero
        low = jnp.where(column != 0, pltpu.roll(tile, 1, 1), 0.0)
        high = jnp.where(column != NY - 1, pltpu.roll(tile, LANES - 1, 1), 0.0)
        left = pltpu.roll(jnp.where(lane < LANES - NY, tile, before), NY, 1)
        right = pltpu.roll(jnp.where(lane >= NY, tile, after), LANES - NY, 1)
        out.append((low + high) + (left + right))
    return jnp.concatenate(out, axis=1)


def lane_fold(value):
    tiles = tiles_of(value)
    while len(tiles) > 1:
        tiles = [sum(tiles[at : at + 2]) for at in range(0, len(tiles), 2)]
    return tiles[0]


def split(value):
    high = value.astype(jnp.bfloat16)
    return high, (value - high.astype(jnp.float32)).astype(jnp.bfloat16)


def kernel(
    count, doms, sliced, total_cells,
    samples, pot, gath, fin,
    sext, pot_near, pe, inv, wd, ua, ub, p1, gram, coef, mext, rhs, red,
    local_sem, halo_send, halo_recv, gram_send, gram_recv, edge_send, edge_recv,
    gath_send, gath_recv, red_send, red_recv, fin_send, fin_recv,
):
    me = lax.axis_index("shift")
    dom = lax.axis_index("dom")
    planes = pot.shape[0]
    cols, cells = sext.shape[1:]
    reps = cells // LANES
    below, above = dom > 0, dom < doms - 1

    barrier = pltpu.get_barrier_semaphore()
    for step in range(1, count):
        pl.semaphore_signal(barrier, inc=1, device_id={"shift": lax.rem(me + step, count)}, device_id_type=MESH)
    for step in range(1, doms):
        pl.semaphore_signal(barrier, inc=1, device_id={"dom": lax.rem(dom + step, doms)}, device_id_type=MESH)

    mine = pl.ds(pl.multiple_of(me * cols, 8), cols) if sliced else pl.ds(0, cols)
    own = pltpu.make_async_copy(samples.at[:, mine, :], sext.at[pl.ds(2, planes)], local_sem)
    own.start()
    pl.semaphore_wait(barrier, count - 1 + doms - 1)

    def halo(first, slot, to, to_slot):
        return (
            pltpu.make_async_remote_copy(
                samples.at[pl.ds(first, 2), mine, :], sext.at[pl.ds(slot, 2)],
                halo_send.at[to_slot, 0], halo_recv.at[to_slot, 0], {"dom": to}, device_id_type=MESH),
            pltpu.make_async_remote_copy(
                pot, pot_near.at[to_slot],
                halo_send.at[to_slot, 1], halo_recv.at[to_slot, 1], {"dom": to}, device_id_type=MESH),
        )

    up = halo(planes - 2, 0, lax.rem(dom + 1, doms), 0)
    down = halo(0, planes + 2, lax.rem(dom + doms - 1, doms), 1)

    @pl.when(above)
    def _():
        for copy in up:
            copy.start()

    @pl.when(below)
    def _():
        for copy in down:
            copy.start()

    @pl.when(jnp.logical_not(below))
    def _():
        sext[0:2] = jnp.zeros((2, cols, cells), jnp.float32)
        pot_near[0] = jnp.zeros((planes, cells), jnp.float32)

    @pl.when(jnp.logical_not(above))
    def _():
        sext[planes + 2 : planes + 4] = jnp.zeros((2, cols, cells), jnp.float32)
        pot_near[1] = jnp.zeros((planes, cells), jnp.float32)

    @pl.when(below)
    def _():
        for copy in up:
            copy.wait_recv()
        for copy in down:
            copy.wait_send()

    @pl.when(above)
    def _():
        for copy in down:
            copy.wait_recv()
        for copy in up:
            copy.wait_send()

    own.wait()
    pe[0:2] = pot_near[0, planes - 2 : planes]
    pe[2 : planes + 2] = pot[...]
    pe[planes + 2 : planes + 4] = pot_near[1, 0:2]

    for node in range(count):
        angle = math.pi * (node + 0.5) / count
        cos, sin = RADIUS * math.cos(angle), RADIUS * math.sin(angle)
        diag = (CENTRE + cos) - (6.0 + pe[...])
        over = 1.0 / (diag * diag + sin * sin)
        inv_re, inv_im = diag * over, -sin * over
        inv[node, 0] = inv_re
        inv[node, 1] = inv_im
        wd[node, 0] = (cos / count) * inv_re - (sin / count) * inv_im
        wd[node, 1] = (cos / count) * inv_im + (sin / count) * inv_re

    width = gram.shape[2]
    lane_at = lax.broadcasted_iota(jnp.int32, (cols, width), 1)

    def row(ref, node, part, at):
        return jnp.broadcast_to(ref[node, part, pl.ds(at, 1), :], (cols, cells))

    def each_node(node, packed):
        def first(at, carry):
            ua[0, at] = sext[at] * row(inv, node, 0, at)
            ua[1, at] = sext[at] * row(inv, node, 1, at)
            return carry

        lax.fori_loop(0, planes + 4, first, 0)

        def second(at, carry):
            p_re = sext[at] + (plane_sum(ua[0, at]) + (ua[0, at - 1] + ua[0, at + 1]))
            p_im = plane_sum(ua[1, at]) + (ua[1, at - 1] + ua[1, at + 1])
            p1[node, 0, at] = p_re
            p1[node, 1, at] = p_im
            i_re, i_im = row(inv, node, 0, at), row(inv, node, 1, at)
            ub[0, at] = p_re * i_re - p_im * i_im
            ub[1, at] = p_re * i_im + p_im * i_re
            return carry

        lax.fori_loop(1, planes + 3, second, 0)

        @pl.when(jnp.logical_not(below))
        def _():
            ub[0, 1] = jnp.zeros((cols, cells), jnp.float32)
            ub[1, 1] = jnp.zeros((cols, cells), jnp.float32)

        @pl.when(jnp.logical_not(above))
        def _():
            ub[0, planes + 2] = jnp.zeros((cols, cells), jnp.float32)
            ub[1, planes + 2] = jnp.zeros((cols, cells), jnp.float32)

        def third(at, sums):
            s = sext[at]
            a_re, a_im = p1[node, 0, at], p1[node, 1, at]
            b_re = a_re + (plane_sum(ub[0, at]) + (ub[0, at - 1] + ub[0, at + 1]))
            b_im = a_im + (plane_sum(ub[1, at]) + (ub[1, at - 1] + ub[1, at + 1]))
            terms = (
                a_re * a_re + a_im * a_im, a_re * s, -a_im * s,
                a_re * b_re + a_im * b_im, a_re * b_im - a_im * b_re,
                b_re * b_re + b_im * b_im, b_re * s, -b_im * s,
            )
            return tuple(old + lane_fold(term) for old, term in zip(sums, terms))

        zero = jnp.zeros((cols, LANES), jnp.float32)
        sums = lax.fori_loop(2, planes + 2, third, (zero,) * 8)
        for at, value in enumerate(sums):
            packed = jnp.where(lane_at == node * 8 + at, jnp.sum(value, axis=1, keepdims=True), packed)
        return packed

    gram[dom] = lax.fori_loop(0, count, each_node, jnp.zeros((cols, width), jnp.float32))

    def to_all(buffer, sends, recvs, axis, place, size):
        out = [
            pltpu.make_async_remote_copy(
                buffer.at[place], buffer.at[place], sends.at[step - 1], recvs.at[step - 1],
                {axis: lax.rem(place + step, size)}, device_id_type=MESH)
            for step in range(1, size)
        ]
        for copy in out:
            copy.start()
        for copy in out:
            copy.wait()

    to_all(gram, gram_send, gram_recv, "dom", dom, doms)
    total = gram[0]
    for other in range(1, doms):
        total = total + gram[other]
    g_one, q_one_re, q_one_im, g_mix_re, g_mix_im, g_two, q_two_re, q_two_im = [
        total if at == 0 else pltpu.roll(total, width - at, 1) for at in range(8)
    ]
    ridge = RIDGE * (g_one + g_two) / 2.0
    determ = (g_one + ridge) * (g_two + ridge) - (g_mix_re * g_mix_re + g_mix_im * g_mix_im)
    coefs = (
        ((g_two + ridge) * q_one_re - (g_mix_re * q_two_re - g_mix_im * q_two_im)) / determ,
        ((g_two + ridge) * q_one_im - (g_mix_re * q_two_im + g_mix_im * q_two_re)) / determ,
        ((g_one + ridge) * q_two_re - (g_mix_re * q_one_re + g_mix_im * q_one_im)) / determ,
        ((g_one + ridge) * q_two_im - (g_mix_re * q_one_im - g_mix_im * q_one_re)) / determ,
    )
    for node in range(count):
        for at, value in enumerate(coefs):
            coef[node, at] = jnp.broadcast_to(value[:, node * 8 : node * 8 + 1], (cols, LANES))

    def wide(node, at):
        return jnp.concatenate([coef[node, at]] * reps, axis=1)

    def moment(at, carry):
        s = sext[at]

        def add(node, value):
            c1r, c1i, c2r, c2i = [wide(node, part) for part in range(4)]
            a_re, a_im = p1[node, 0, at], p1[node, 1, at]
            y_re = c1r * s + c2r * a_re - c2i * a_im
            y_im = c1i * s + c2r * a_im + c2i * a_re
            return value + (row(wd, node, 0, at) * y_re - row(wd, node, 1, at) * y_im)

        value = lax.fori_loop(0, count, add, jnp.zeros((cols, cells), jnp.float32), unroll=2)
        mext[at - 1] = value
        gath[me, at - 2] = value
        rhs[at - 2, cols:] = value
        return carry

    lax.fori_loop(2, planes + 2, moment, 0)

    bits = [1 << at for at in range(count.bit_length() - 1)]
    orders = [bits[1:] + bits[:1], bits[1:][::-1] + bits[:1]]
    half = planes // 2

    def last_of(gap, order):
        return max([at for at, bit in enumerate(order) if gap & bit], default=-1)

    def hop(gap, part, at):
        bit = orders[part][at]
        where = lax.bitwise_xor(me, gap)
        block = gath.at[where, pl.ds(part * half, half if part == 0 else planes - half)]
        return pltpu.make_async_remote_copy(
            block, block, gath_send.at[part, gap, at], gath_recv.at[part, gap | bit],
            {"shift": lax.bitwise_xor(me, bit)}, device_id_type=MESH)

    def forward(gap, part, only=None):
        for at in range(last_of(gap, orders[part]) + 1, len(bits)):
            hop(gap, part, at).start()

    def arrived(gap, part):
        at = last_of(gap, orders[part])
        before = gap & ~orders[part][at]
        bit = orders[part][at]
        where = lax.bitwise_xor(me, gap)
        block = gath.at[where, pl.ds(part * half, half if part == 0 else planes - half)]
        pltpu.make_async_remote_copy(
            block, block, gath_send.at[part, before, at], gath_recv.at[part, gap],
            {"shift": lax.bitwise_xor(me, bit)}, device_id_type=MESH).wait_recv()

    def edge(plane, slot, to, to_slot):
        return pltpu.make_async_remote_copy(
            mext.at[plane], mext.at[slot], edge_send.at[to_slot], edge_recv.at[to_slot],
            {"dom": to}, device_id_type=MESH)

    edge_up = edge(planes, 0, lax.rem(dom + 1, doms), 0)
    edge_down = edge(1, planes + 1, lax.rem(dom + doms - 1, doms), 1)

    @pl.when(above)
    def _():
        edge_up.start()

    @pl.when(below)
    def _():
        edge_down.start()

    for part in range(2):
        forward(0, part)

    @pl.when(jnp.logical_not(below))
    def _():
        mext[0] = jnp.zeros((cols, cells), jnp.float32)

    @pl.when(jnp.logical_not(above))
    def _():
        mext[planes + 1] = jnp.zeros((cols, cells), jnp.float32)

    @pl.when(below)
    def _():
        edge_up.wait_recv()
        edge_down.wait_send()

    @pl.when(above)
    def _():
        edge_down.wait_recv()
        edge_up.wait_send()

    def apply(at, carry):
        onsite = 6.0 + jnp.broadcast_to(pe[pl.ds(at + 1, 1), :], (cols, cells))
        value = mext[at]
        rhs[at - 1, :cols] = onsite * value - (plane_sum(value) + (mext[at - 1] + mext[at + 1]))
        return carry

    lax.fori_loop(1, planes + 1, apply, 0)

    arrivals = sorted(
        ((gap, part) for gap in range(1, count) for part in range(2)),
        key=lambda pair: (pair[0] & 1, bin(pair[0]).count("1"), last_of(pair[0], orders[pair[1]]), pair[1]))
    for gap, part in arrivals:
        arrived(gap, part)
        forward(gap, part)

    def contract(at, value):
        left_hi, left_lo = split(rhs[at])
        right_hi, right_lo = split(gath[:, at].reshape(count * cols, cells))
        dims = (((1,), (1,)), ((), ()))
        dot = functools.partial(lax.dot_general, dimension_numbers=dims, preferred_element_type=jnp.float32)
        return value + (dot(left_hi, right_hi) + (dot(left_hi, right_lo) + dot(left_lo, right_hi)))

    value = lax.fori_loop(0, planes, contract, jnp.zeros((2 * cols, count * cols), jnp.float32))
    red[dom] = value
    to_all(red, red_send, red_recv, "dom", dom, doms)
    total = red[0]
    for other in range(1, doms):
        total = total + red[other]
    fin[me] = total * (1.0 / total_cells)
    to_all(fin, fin_send, fin_recv, "shift", me, count)

    for part in range(2):
        for gap in range(count):
            for at in range(last_of(gap, orders[part]) + 1, len(bits)):
                hop(gap, part, at).wait_send()


def on_device(count, doms, samples, potential):
    planes, vectors, cells = samples.shape
    own = vectors // count
    cols = -(-own // 8) * 8
    sliced = own == cols
    if not sliced:
        part = lax.dynamic_slice_in_dim(samples, lax.axis_index("shift") * own, own, axis=1)
        samples = jnp.pad(part, ((0, 0), (0, cols - own), (0, 0)))
    width = -(-count * 8 // LANES) * LANES
    levels = count.bit_length() - 1
    f32 = jnp.float32
    dma = pltpu.SemaphoreType.DMA
    vmem = pl.BlockSpec(memory_space=pltpu.VMEM)
    gath, fin = pl.pallas_call(
        functools.partial(kernel, count, doms, sliced, planes * doms * cells),
        out_shape=(
            jax.ShapeDtypeStruct((count, planes, cols, cells), f32),
            jax.ShapeDtypeStruct((count, 2 * cols, count * cols), f32),
        ),
        in_specs=[pl.BlockSpec(memory_space=pl.ANY), vmem],
        out_specs=(vmem, vmem),
        scratch_shapes=[
            pltpu.VMEM((planes + 4, cols, cells), f32),
            pltpu.VMEM((2, planes, cells), f32),
            pltpu.VMEM((planes + 4, cells), f32),
            pltpu.VMEM((count, 2, planes + 4, cells), f32),
            pltpu.VMEM((count, 2, planes + 4, cells), f32),
            pltpu.VMEM((2, planes + 4, cols, cells), f32),
            pltpu.VMEM((2, planes + 4, cols, cells), f32),
            pltpu.VMEM((count, 2, planes + 4, cols, cells), f32),
            pltpu.VMEM((doms, cols, width), f32),
            pltpu.VMEM((count, 4, cols, LANES), f32),
            pltpu.VMEM((planes + 2, cols, cells), f32),
            pltpu.VMEM((planes, 2 * cols, cells), f32),
            pltpu.VMEM((doms, 2 * cols, count * cols), f32),
            dma,
            dma((2, 2)), dma((2, 2)),
            dma((doms,)), dma((doms,)),
            dma((2,)), dma((2,)),
            dma((2, count, levels)), dma((2, count)),
            dma((doms,)), dma((doms,)),
            dma((count,)), dma((count,)),
        ],
        compiler_params=pltpu.CompilerParams(
            collective_id=0, has_side_effects=True, vmem_limit_bytes=56 * 1024 * 1024
        ),
        name="feast_step",
    )(samples, potential)
    subspace = jnp.transpose(gath[:, :, :own], (1, 0, 2, 3)).reshape(planes, vectors, cells)
    fin = fin.reshape(count, 2, cols, count, cols)[:, :, :own, :, :own]
    fin = jnp.transpose(fin, (1, 3, 4, 0, 2)).reshape(2, vectors, vectors)
    return subspace, fin[0], fin[1]


def solution(mesh):
    in_specs = (P("dom", None, None), P("dom", None))
    out_specs = (P("dom", None, None), P(), P())
    return jax.shard_map(
        functools.partial(on_device, mesh.shape["shift"], mesh.shape["dom"]),
        mesh=mesh, in_specs=in_specs, out_specs=out_specs, check_vma=False,
    )
```

time: 186 us -> 66.1 us (0.36)
  waiting for transfers between devices: 73.8 us -> 0 us
  Pallas kernels: 0 us -> 60.2 us
  other arithmetic: 38.1 us -> 0 us
  blocking collectives: 31.5 us -> 0 us
  between operations: 14.5 us -> 0.68 us
  starting transfers between devices: 12.2 us -> 0 us
  matrix products: 7.85 us -> 0 us
  local copies, waits for them, and re-layouts: 7.97 us -> 5.06 us
    psum x1 -> x0, waiting for transfers between devices: 60.2 us -> none  [on_device(): subspace = lax.psum(weighted, 'shift')]
    pallas_call x0 -> x1, Pallas kernels: none -> 60.2 us  [on_device(): pl.pallas_call(functools.partial(kernel, count, doms, sliced, planes * do...]
    psum x2 -> x0, blocking collectives: 31.5 us -> none  [the longest x1 21.2 us: on_device(): reduced_h, reduced_b = lax.psum((part_h, part_b), 'dom')]
    sub x6 -> x0, other arithmetic: 28.5 us -> none  [the longest x2 18.2 us: shrink_operate(): return combine(inner, onsite_inner * inner - beside)]
    ppermute x4 -> x0, waiting for transfers between devices: 13.5 us -> none  [the longest x2 8.03 us: extended_2(): before = lax.ppermute(last, axis, up)]
    ppermute x4 -> x0, starting transfers between devices: 12.1 us -> none  [the longest x2 9.55 us: extended_2(): before = lax.ppermute(last, axis, up)]
    dot_general x2 -> x0, matrix products: 7.85 us -> none  [the longest x1 4.03 us: on_device(): jnp.einsum('znc,zmc->nm', subspace, subspace, precision=lax.Precision.HIG...]
    another operation x5 -> x0, other arithmetic: 4.3 us -> none  [the longest x3 4.26 us: apply_inv(): jnp.stack([vector[0] * inv_pair[0] - vector[1] * inv_pair[1], vector[0] *...]
  transfers between devices with their start and end apart: 5 -> 0, of which waited for: 3 -> 0; matrix products, arithmetic and copies ran while one was open for 3% -> 0% of each run, Pallas kernels for 0% -> 0%
where the time goes in v1:
time: 66.1 us; the launch traced here: 65.9 us
  Pallas kernels  60.2 us (91%)
  local copies, waits for them, and re-layouts  5.06 us (8%)
  between operations  0.68 us (1%)
    pallas_call x1, Pallas kernels, on_device(): pl.pallas_call(functools.partial(kernel, count, doms, sliced, planes * do...  60.2 us
    reshape x1, local copies, waits for them, and re-layouts, on_device(): jnp.transpose(gath[:, :, :own], (1, 0, 2, 3))  3.19 us
    squeeze x4, local copies, waits for them, and re-layouts, on_device(): return (subspace, fin[0], fin[1])  1.65 us

profile of v1, /device:TPU:0, one launch (start us, length us, event | category | flops | bytes accessed | tf_op | source)
XLA Modules:
  0.0 65.9 jit_solution(13986538728162881490)
XLA Ops:
  0.6 60.2 %feast_step.1 = (f32[8,8,8,1024]{3,2,1,0:T(8,128)}, f32[8,16,64]{2,1,0:T(8,128)}) custom-call(f32[8,64,1024]{2,1,0:T(8,128)} %samples.1, f32[8,1024]{1,0:T(8,128)} %pot.1), custom_call_target="tpu_custom_call" | custom-call | tf_op jit(solution)/shard_map/feast_step/pallas_call | solution.py:366
  60.8 0.0 copy-start
  60.8 3.2 %copy_bitcast_fusion = f32[8,64,1024]{2,1,0:T(8,128)} fusion(f32[8,8,8,1024]{3,2,1,0:T(8,128)} %get-tuple-element.5), kind=kLoop, calls=%fused_computation | loop fusion | bytes 4194304 | tf_op jit(solution)/shard_map/reshape | solution.py:401
  64.0 0.0 copy-done
  64.0 0.2 reshape.18
  64.3 0.1 reshape.20
  64.4 0.7 %copy.11 = f32[64,64]{1,0:T(8,128)} copy(f32[64,64]{0,1:T(8,128)S(1)} %reshape.20) | data formatting | bytes 32768 | tf_op jit(solution)/shard_map/squeeze | solution.py:404
  65.1 0.1 reshape.19
  65.2 0.7 %copy.10 = f32[64,64]{1,0:T(8,128)} copy(f32[64,64]{0,1:T(8,128)S(1)} %reshape.19) | data formatting | bytes 32768 | tf_op jit(solution)/shard_map/squeeze | solution.py:404
  (1 shorter events, 0.0 us)
Async XLA Ops:
  60.8 3.2 %copy-start = (f32[8,16,64]{2,1,0:T(8,128)S(1)}, f32[8,16,64]{2,1,0:T(8,128)}, u32[]{:S(2)}) copy-start(f32[8,16,64]{2,1,0:T(8,128)} %get-tuple-element.6) | copy-start | bytes 98308

commit v2 on v1

--- a/solution.py
+++ b/solution.py
@@ -22,28 +22,55 @@
     return [value[:, at : at + LANES] for at in range(0, value.shape[1], LANES)]
 
 
-def plane_sum(value):
-    tiles = tiles_of(value)
-    lane = lax.broadcasted_iota(jnp.int32, tiles[0].shape, 1)
+def lane_of(value):
+    return lax.broadcasted_iota(jnp.int32, value.shape, 1)
+
+
+def spread(tiles):
+    count, per = len(tiles), LANES // NY
+    block = lane_of(tiles[0]) // NY
+    out = []
+    for at in range(count):
+        for to in range(per):
+            x = to * count + at
+            part = tiles[x // per]
+            move = (NY * (to - x % per)) % LANES
+            part = pltpu.roll(part, move, 1) if move else part
+            value = part if to == 0 else jnp.where(block == to, part, value)
+        out.append(value)
+    return out
+
+
+def gather_back(tiles):
+    count, per = len(tiles), LANES // NY
+    block = lane_of(tiles[0]) // NY
+    out = []
+    for at in range(count):
+        for to in range(per):
+            x = at * per + to
+            part = tiles[x % count]
+            move = (NY * (to - x // count)) % LANES
+            part = pltpu.roll(part, move, 1) if move else part
+            value = part if to == 0 else jnp.where(block == to, part, value)
+        out.append(value)
+    return out
+
+
+def neighbours(get, at, tile, count):
+    here = get(at, tile)
+    lane = lane_of(here)
     column = lane % NY
-    zero = jnp.zeros_like(tiles[0])
-    out = []
-    for at, tile in enumerate(tiles):
-        before = tiles[at - 1] if at > 0 else zero
-        after = tiles[at + 1] if at + 1 < len(tiles) else zero
-        low = jnp.where(column != 0, pltpu.roll(tile, 1, 1), 0.0)
-        high = jnp.where(column != NY - 1, pltpu.roll(tile, LANES - 1, 1), 0.0)
-        left = pltpu.roll(jnp.where(lane < LANES - NY, tile, before), NY, 1)
-        right = pltpu.roll(jnp.where(lane >= NY, tile, after), LANES - NY, 1)
-        out.append((low + high) + (left + right))
-    return jnp.concatenate(out, axis=1)
-
-
-def lane_fold(value):
-    tiles = tiles_of(value)
-    while len(tiles) > 1:
-        tiles = [sum(tiles[at : at + 2]) for at in range(0, len(tiles), 2)]
-    return tiles[0]
+    low = jnp.where(column != 0, pltpu.roll(here, 1, 1), 0.0)
+    high = jnp.where(column != NY - 1, pltpu.roll(here, LANES - 1, 1), 0.0)
+    if tile > 0:
+        left = get(at, tile - 1)
+    else:
+        left = jnp.where(lane >= NY, pltpu.roll(get(at, count - 1), NY, 1), 0.0)
+    if tile < count - 1:
+        right = get(at, tile + 1)
+    else:
+        right = jnp.where(lane < LANES - NY, pltpu.roll(get(at, 0), LANES - NY, 1), 0.0)
+    return ((low + high) + (left + right)) + (get(at - 1, tile) + get(at + 1, tile))
 
 
 def split(value):
@@ -54,7 +81,7 @@
 def kernel(
     count, doms, sliced, total_cells,
     samples, pot, gath, fin,
-    sext, pot_near, pe, inv, wd, ua, ub, p1, gram, coef, mext, rhs, red,
+    sraw, sext, pot_near, pe, inv, wd, ua, ub, p1, gram, coef, mext, rhs, red,
     local_sem, halo_send, halo_recv, gram_send, gram_recv, edge_send, edge_recv,
     gath_send, gath_recv, red_send, red_recv, fin_send, fin_recv,
 ):
@@ -65,6 +92,10 @@
     reps = cells // LANES
     below, above = dom > 0, dom < doms - 1
 
+    def lanes(tile):
+        return pl.ds(tile * LANES, LANES)
+
+
     barrier = pltpu.get_barrier_semaphore()
     for step in range(1, count):
         pl.semaphore_signal(barrier, inc=1, device_id={"shift": lax.rem(me + step, count)}, device_id_type=MESH)
@@ -72,14 +103,14 @@
         pl.semaphore_signal(barrier, inc=1, device_id={"dom": lax.rem(dom + step, doms)}, device_id_type=MESH)
 
     mine = pl.ds(pl.multiple_of(me * cols, 8), cols) if sliced else pl.ds(0, cols)
-    own = pltpu.make_async_copy(samples.at[:, mine, :], sext.at[pl.ds(2, planes)], local_sem)
+    own = pltpu.make_async_copy(samples.at[:, mine, :], sraw.at[pl.ds(2, planes)], local_sem)
     own.start()
     pl.semaphore_wait(barrier, count - 1 + doms - 1)
 
     def halo(first, slot, to, to_slot):
         return (
             pltpu.make_async_remote_copy(
-                samples.at[pl.ds(first, 2), mine, :], sext.at[pl.ds(slot, 2)],
+                samples.at[pl.ds(first, 2), mine, :], sraw.at[pl.ds(slot, 2)],
                 halo_send.at[to_slot, 0], halo_recv.at[to_slot, 0], {"dom": to}, device_id_type=MESH),
             pltpu.make_async_remote_copy(
                 pot, pot_near.at[to_slot],
@@ -101,12 +132,12 @@
 
     @pl.when(jnp.logical_not(below))
     def _():
-        sext[0:2] = jnp.zeros((2, cols, cells), jnp.float32)
+        sraw[0:2] = jnp.zeros((2, cols, cells), jnp.float32)
         pot_near[0] = jnp.zeros((planes, cells), jnp.float32)
 
     @pl.when(jnp.logical_not(above))
     def _():
-        sext[planes + 2 : planes + 4] = jnp.zeros((2, cols, cells), jnp.float32)
+        sraw[planes + 2 : planes + 4] = jnp.zeros((2, cols, cells), jnp.float32)
         pot_near[1] = jnp.zeros((planes, cells), jnp.float32)
 
     @pl.when(below)
@@ -127,6 +158,16 @@
     pe[0:2] = pot_near[0, planes - 2 : planes]
     pe[2 : planes + 2] = pot[...]
     pe[planes + 2 : planes + 4] = pot_near[1, 0:2]
+
+    for at, tile in enumerate(spread(tiles_of(pe[...]))):
+        pe[:, lanes(at)] = tile
+
+    def spread_plane(at, carry):
+        for tile, value in enumerate(spread(tiles_of(sraw[at]))):
+            sext[at, :, lanes(tile)] = value
+        return carry
+
+    lax.fori_loop(0, planes + 4, spread_plane, 0)
 
     for node in range(count):
         angle = math.pi * (node + 0.5) / count
@@ -142,28 +183,42 @@
     width = gram.shape[2]
     lane_at = lax.broadcasted_iota(jnp.int32, (cols, width), 1)
 
-    def row(ref, node, part, at):
-        return jnp.broadcast_to(ref[node, part, pl.ds(at, 1), :], (cols, cells))
+    def row(ref, node, part, at, tile):
+        return jnp.broadcast_to(ref[node, part, at : at + 1, lanes(tile)], (cols, LANES))
+
+    def field(ref, part, centre):
+        seen = {}
+
+        def get(shift, tile):
+            if (shift, tile) not in seen:
+                seen[shift, tile] = ref[part, centre + shift, :, lanes(tile)]
+            return seen[shift, tile]
+
+        return get
 
     def each_node(node, packed):
-        def first(at, carry):
-            ua[0, at] = sext[at] * row(inv, node, 0, at)
-            ua[1, at] = sext[at] * row(inv, node, 1, at)
-            return carry
-
-        lax.fori_loop(0, planes + 4, first, 0)
-
-        def second(at, carry):
-            p_re = sext[at] + (plane_sum(ua[0, at]) + (ua[0, at - 1] + ua[0, at + 1]))
-            p_im = plane_sum(ua[1, at]) + (ua[1, at - 1] + ua[1, at + 1])
-            p1[node, 0, at] = p_re
-            p1[node, 1, at] = p_im
-            i_re, i_im = row(inv, node, 0, at), row(inv, node, 1, at)
-            ub[0, at] = p_re * i_re - p_im * i_im
-            ub[1, at] = p_re * i_im + p_im * i_re
-            return carry
-
-        lax.fori_loop(1, planes + 3, second, 0)
+        def first(at):
+            for tile in range(reps):
+                s = sext[at, :, lanes(tile)]
+                ua[0, at, :, lanes(tile)] = s * row(inv, node, 0, at, tile)
+                ua[1, at, :, lanes(tile)] = s * row(inv, node, 1, at, tile)
+
+        for at in range(0, planes + 4):
+            first(at)
+
+        def second(at):
+            u_re, u_im = field(ua, 0, at), field(ua, 1, at)
+            for tile in range(reps):
+                p_re = sext[at, :, lanes(tile)] + neighbours(u_re, 0, tile, reps)
+                p_im = neighbours(u_im, 0, tile, reps)
+                p1[node, 0, at, :, lanes(tile)] = p_re
+                p1[node, 1, at, :, lanes(tile)] = p_im
+                i_re, i_im = row(inv, node, 0, at, tile), row(inv, node, 1, at, tile)
+                ub[0, at, :, lanes(tile)] = p_re * i_re - p_im * i_im
+                ub[1, at, :, lanes(tile)] = p_re * i_im + p_im * i_re
+
+        for at in range(1, planes + 3):
+            second(at)
 
         @pl.when(jnp.logical_not(below))
         def _():
@@ -176,16 +231,19 @@
             ub[1, planes + 2] = jnp.zeros((cols, cells), jnp.float32)
 
         def third(at, sums):
-            s = sext[at]
-            a_re, a_im = p1[node, 0, at], p1[node, 1, at]
-            b_re = a_re + (plane_sum(ub[0, at]) + (ub[0, at - 1] + ub[0, at + 1]))
-            b_im = a_im + (plane_sum(ub[1, at]) + (ub[1, at - 1] + ub[1, at + 1]))
-            terms = (
-                a_re * a_re + a_im * a_im, a_re * s, -a_im * s,
-                a_re * b_re + a_im * b_im, a_re * b_im - a_im * b_re,
-                b_re * b_re + b_im * b_im, b_re * s, -b_im * s,
-            )
-            return tuple(old + lane_fold(term) for old, term in zip(sums, terms))
+            u_re, u_im = field(ub, 0, at), field(ub, 1, at)
+            for tile in range(reps):
+                s = sext[at, :, lanes(tile)]
+                a_re, a_im = p1[node, 0, at, :, lanes(tile)], p1[node, 1, at, :, lanes(tile)]
+                b_re = a_re + neighbours(u_re, 0, tile, reps)
+                b_im = a_im + neighbours(u_im, 0, tile, reps)
+                terms = (
+                    a_re * a_re + a_im * a_im, a_re * s, -(a_im * s),
+                    a_re * b_re + a_im * b_im, a_re * b_im - a_im * b_re,
+                    b_re * b_re + b_im * b_im, b_re * s, -(b_im * s),
+                )
+                sums = tuple(old + term for old, term in zip(sums, terms))
+            return sums
 
         zero = jnp.zeros((cols, LANES), jnp.float32)
         sums = lax.fori_loop(2, planes + 2, third, (zero,) * 8)
@@ -226,26 +284,25 @@
         for at, value in enumerate(coefs):
             coef[node, at] = jnp.broadcast_to(value[:, node * 8 : node * 8 + 1], (cols, LANES))
 
-    def wide(node, at):
-        return jnp.concatenate([coef[node, at]] * reps, axis=1)
-
-    def moment(at, carry):
-        s = sext[at]
-
-        def add(node, value):
-            c1r, c1i, c2r, c2i = [wide(node, part) for part in range(4)]
-            a_re, a_im = p1[node, 0, at], p1[node, 1, at]
-            y_re = c1r * s + c2r * a_re - c2i * a_im
-            y_im = c1i * s + c2r * a_im + c2i * a_re
-            return value + (row(wd, node, 0, at) * y_re - row(wd, node, 1, at) * y_im)
-
-        value = lax.fori_loop(0, count, add, jnp.zeros((cols, cells), jnp.float32), unroll=2)
-        mext[at - 1] = value
-        gath[me, at - 2] = value
-        rhs[at - 2, cols:] = value
-        return carry
-
-    lax.fori_loop(2, planes + 2, moment, 0)
+    def moment(at):
+        values = [jnp.zeros((cols, LANES), jnp.float32)] * reps
+        for node in range(count):
+            c1r, c1i, c2r, c2i = [coef[node, part] for part in range(4)]
+            for tile in range(reps):
+                s = sext[at, :, lanes(tile)]
+                a_re, a_im = p1[node, 0, at, :, lanes(tile)], p1[node, 1, at, :, lanes(tile)]
+                y_re = c1r * s + (c2r * a_re - c2i * a_im)
+                y_im = c1i * s + (c2r * a_im + c2i * a_re)
+                values[tile] = values[tile] + (
+                    row(wd, node, 0, at, tile) * y_re - row(wd, node, 1, at, tile) * y_im)
+        for tile, value in enumerate(values):
+            mext[0, at - 1, :, lanes(tile)] = value
+        for tile, value in enumerate(gather_back(values)):
+            gath[me, at - 2, :, lanes(tile)] = value
+            rhs[at - 2, cols:, lanes(tile)] = value
+
+    for at in range(2, planes + 2):
+        moment(at)
 
     bits = [1 << at for at in range(count.bit_length() - 1)]
     orders = [bits[1:] + bits[:1], bits[1:][::-1] + bits[:1]]
@@ -278,7 +335,7 @@
 
     def edge(plane, slot, to, to_slot):
         return pltpu.make_async_remote_copy(
-            mext.at[plane], mext.at[slot], edge_send.at[to_slot], edge_recv.at[to_slot],
+            mext.at[0, plane], mext.at[0, slot], edge_send.at[to_slot], edge_recv.at[to_slot],
             {"dom": to}, device_id_type=MESH)
 
     edge_up = edge(planes, 0, lax.rem(dom + 1, doms), 0)
@@ -297,11 +354,11 @@
 
     @pl.when(jnp.logical_not(below))
     def _():
-        mext[0] = jnp.zeros((cols, cells), jnp.float32)
+        mext[0, 0] = jnp.zeros((cols, cells), jnp.float32)
 
     @pl.when(jnp.logical_not(above))
     def _():
-        mext[planes + 1] = jnp.zeros((cols, cells), jnp.float32)
+        mext[0, planes + 1] = jnp.zeros((cols, cells), jnp.float32)
 
     @pl.when(below)
     def _():
@@ -313,13 +370,17 @@
         edge_down.wait_recv()
         edge_up.wait_send()
 
-    def apply(at, carry):
-        onsite = 6.0 + jnp.broadcast_to(pe[pl.ds(at + 1, 1), :], (cols, cells))
-        value = mext[at]
-        rhs[at - 1, :cols] = onsite * value - (plane_sum(value) + (mext[at - 1] + mext[at + 1]))
-        return carry
-
-    lax.fori_loop(1, planes + 1, apply, 0)
+    def apply(at):
+        get = field(mext, 0, at)
+        values = []
+        for tile in range(reps):
+            onsite = 6.0 + jnp.broadcast_to(pe[at + 1 : at + 2, lanes(tile)], (cols, LANES))
+            values.append(onsite * get(0, tile) - neighbours(get, 0, tile, reps))
+        for tile, value in enumerate(gather_back(values)):
+            rhs[at - 1, :cols, lanes(tile)] = value
+
+    for at in range(1, planes + 1):
+        apply(at)
 
     arrivals = sorted(
         ((gap, part) for gap in range(1, count) for part in range(2)),
@@ -373,6 +434,7 @@
         out_specs=(vmem, vmem),
         scratch_shapes=[
             pltpu.VMEM((planes + 4, cols, cells), f32),
+            pltpu.VMEM((planes + 4, cols, cells), f32),
             pltpu.VMEM((2, planes, cells), f32),
             pltpu.VMEM((planes + 4, cells), f32),
             pltpu.VMEM((count, 2, planes + 4, cells), f32),
@@ -382,7 +444,7 @@
             pltpu.VMEM((count, 2, planes + 4, cols, cells), f32),
             pltpu.VMEM((doms, cols, width), f32),
             pltpu.VMEM((count, 4, cols, LANES), f32),
-            pltpu.VMEM((planes + 2, cols, cells), f32),
+            pltpu.VMEM((1, planes + 2, cols, cells), f32),
             pltpu.VMEM((planes, 2 * cols, cells), f32),
             pltpu.VMEM((doms, 2 * cols, count * cols), f32),
             dma,

time: 66.1 us -> 55.9 us (0.85)
  Pallas kernels: 60.2 us -> 50 us
    pallas_call x1, Pallas kernels: 60.2 us -> 50 us  [on_device(): pl.pallas_call(functools.partial(kernel, count, doms, sliced, planes * do...]
where the time goes in v2:
time: 55.9 us; the launch traced here: 55.7 us
  Pallas kernels  50 us (89%)
  local copies, waits for them, and re-layouts  5.06 us (9%)
  between operations  0.68 us (1%)
    pallas_call x1, Pallas kernels, on_device(): pl.pallas_call(functools.partial(kernel, count, doms, sliced, planes * do...  50 us
    reshape x1, local copies, waits for them, and re-layouts, on_device(): jnp.transpose(gath[:, :, :own], (1, 0, 2, 3))  3.19 us
    squeeze x4, local copies, waits for them, and re-layouts, on_device(): return (subspace, fin[0], fin[1])  1.65 us

profile of v2, /device:TPU:0, one launch (start us, length us, event | category | flops | bytes accessed | tf_op | source)
XLA Modules:
  0.0 55.7 jit_solution(5653980005850770948)
XLA Ops:
  0.6 50.0 %feast_step.1 = (f32[8,8,8,1024]{3,2,1,0:T(8,128)}, f32[8,16,64]{2,1,0:T(8,128)}) custom-call(f32[8,64,1024]{2,1,0:T(8,128)} %samples.1, f32[8,1024]{1,0:T(8,128)} %pot.1), custom_call_target="tpu_custom_call" | custom-call | tf_op jit(solution)/shard_map/feast_step/pallas_call | solution.py:427
  50.6 0.0 copy-start
  50.6 3.2 %copy_bitcast_fusion = f32[8,64,1024]{2,1,0:T(8,128)} fusion(f32[8,8,8,1024]{3,2,1,0:T(8,128)} %get-tuple-element.5), kind=kLoop, calls=%fused_computation | loop fusion | bytes 4194304 | tf_op jit(solution)/shard_map/reshape | solution.py:463
  53.8 0.0 copy-done
  53.8 0.2 reshape.18
  54.0 0.1 reshape.20
  54.2 0.7 %copy.11 = f32[64,64]{1,0:T(8,128)} copy(f32[64,64]{0,1:T(8,128)S(1)} %reshape.20) | data formatting | bytes 32768 | tf_op jit(solution)/shard_map/squeeze | solution.py:466
  54.9 0.1 reshape.19
  55.0 0.7 %copy.10 = f32[64,64]{1,0:T(8,128)} copy(f32[64,64]{0,1:T(8,128)S(1)} %reshape.19) | data formatting | bytes 32768 | tf_op jit(solution)/shard_map/squeeze | solution.py:466
  (1 shorter events, 0.0 us)
Async XLA Ops:
  50.6 3.2 %copy-start = (f32[8,16,64]{2,1,0:T(8,128)S(1)}, f32[8,16,64]{2,1,0:T(8,128)}, u32[]{:S(2)}) copy-start(f32[8,16,64]{2,1,0:T(8,128)} %get-tuple-element.6) | copy-start | bytes 98308

commit v3 on v2

--- a/solution.py
+++ b/solution.py
@@ -80,10 +80,11 @@
 
 def kernel(
     count, doms, sliced, total_cells,
-    samples, pot, gath, fin,
+    samples, pot, out, out_h, out_b,
+    gath, fin,
     sraw, sext, pot_near, pe, inv, wd, ua, ub, p1, gram, coef, mext, rhs, red,
     local_sem, halo_send, halo_recv, gram_send, gram_recv, edge_send, edge_recv,
-    gath_send, gath_recv, red_send, red_recv, fin_send, fin_recv,
+    gath_send, gath_recv, out_sem, red_send, red_recv, fin_send, fin_recv,
 ):
     me = lax.axis_index("shift")
     dom = lax.axis_index("dom")
@@ -140,51 +141,40 @@
         sraw[planes + 2 : planes + 4] = jnp.zeros((2, cols, cells), jnp.float32)
         pot_near[1] = jnp.zeros((planes, cells), jnp.float32)
 
-    @pl.when(below)
-    def _():
-        for copy in up:
-            copy.wait_recv()
-        for copy in down:
-            copy.wait_send()
-
-    @pl.when(above)
-    def _():
-        for copy in down:
-            copy.wait_recv()
-        for copy in up:
-            copy.wait_send()
-
-    own.wait()
-    pe[0:2] = pot_near[0, planes - 2 : planes]
-    pe[2 : planes + 2] = pot[...]
-    pe[planes + 2 : planes + 4] = pot_near[1, 0:2]
-
-    for at, tile in enumerate(spread(tiles_of(pe[...]))):
-        pe[:, lanes(at)] = tile
+    def row_at(at):
+        if at < 2:
+            return planes + at
+        return at - 2 if at < planes + 2 else at
+
+    def diagonals(rows):
+        for tile, value in enumerate(spread(tiles_of(pe[rows]))):
+            pe[rows, lanes(tile)] = value
+        for node in range(count):
+            angle = math.pi * (node + 0.5) / count
+            cos, sin = RADIUS * math.cos(angle), RADIUS * math.sin(angle)
+            diag = (CENTRE + cos) - (6.0 + pe[rows])
+            over = 1.0 / (diag * diag + sin * sin)
+            inv_re, inv_im = diag * over, -sin * over
+            inv[node, 0, rows] = inv_re
+            inv[node, 1, rows] = inv_im
+            wd[node, 0, rows] = (cos / count) * inv_re - (sin / count) * inv_im
+            wd[node, 1, rows] = (cos / count) * inv_im + (sin / count) * inv_re
 
     def spread_plane(at, carry):
         for tile, value in enumerate(spread(tiles_of(sraw[at]))):
             sext[at, :, lanes(tile)] = value
         return carry
 
-    lax.fori_loop(0, planes + 4, spread_plane, 0)
-
-    for node in range(count):
-        angle = math.pi * (node + 0.5) / count
-        cos, sin = RADIUS * math.cos(angle), RADIUS * math.sin(angle)
-        diag = (CENTRE + cos) - (6.0 + pe[...])
-        over = 1.0 / (diag * diag + sin * sin)
-        inv_re, inv_im = diag * over, -sin * over
-        inv[node, 0] = inv_re
-        inv[node, 1] = inv_im
-        wd[node, 0] = (cos / count) * inv_re - (sin / count) * inv_im
-        wd[node, 1] = (cos / count) * inv_im + (sin / count) * inv_re
+    pe[0:planes] = pot[...]
+    diagonals(slice(0, planes))
+    own.wait()
+    lax.fori_loop(2, planes + 2, spread_plane, 0)
 
     width = gram.shape[2]
     lane_at = lax.broadcasted_iota(jnp.int32, (cols, width), 1)
 
     def row(ref, node, part, at, tile):
-        return jnp.broadcast_to(ref[node, part, at : at + 1, lanes(tile)], (cols, LANES))
+        return jnp.broadcast_to(ref[node, part, row_at(at) : row_at(at) + 1, lanes(tile)], (cols, LANES))
 
     def field(ref, part, centre):
         seen = {}
@@ -196,42 +186,73 @@
 
         return get
 
-    def each_node(node, packed):
+    edge_planes = (1, 2, planes + 1, planes + 2)
+
+    def inner(node, carry):
+        one_node(node, range(2, planes + 2), range(3, planes + 1))
+        return carry
+
+    def one_node(node, firsts, seconds):
         def first(at):
             for tile in range(reps):
                 s = sext[at, :, lanes(tile)]
-                ua[0, at, :, lanes(tile)] = s * row(inv, node, 0, at, tile)
-                ua[1, at, :, lanes(tile)] = s * row(inv, node, 1, at, tile)
-
-        for at in range(0, planes + 4):
-            first(at)
+                ua[node, 0, at, :, lanes(tile)] = s * row(inv, node, 0, at, tile)
+                ua[node, 1, at, :, lanes(tile)] = s * row(inv, node, 1, at, tile)
+
 
         def second(at):
-            u_re, u_im = field(ua, 0, at), field(ua, 1, at)
+            u_re, u_im = field(ua.at[node], 0, at), field(ua.at[node], 1, at)
             for tile in range(reps):
                 p_re = sext[at, :, lanes(tile)] + neighbours(u_re, 0, tile, reps)
                 p_im = neighbours(u_im, 0, tile, reps)
                 p1[node, 0, at, :, lanes(tile)] = p_re
                 p1[node, 1, at, :, lanes(tile)] = p_im
                 i_re, i_im = row(inv, node, 0, at, tile), row(inv, node, 1, at, tile)
-                ub[0, at, :, lanes(tile)] = p_re * i_re - p_im * i_im
-                ub[1, at, :, lanes(tile)] = p_re * i_im + p_im * i_re
-
-        for at in range(1, planes + 3):
+                ub[node, 0, at, :, lanes(tile)] = p_re * i_re - p_im * i_im
+                ub[node, 1, at, :, lanes(tile)] = p_re * i_im + p_im * i_re
+
+        for at in firsts:
+            first(at)
+        for at in seconds:
             second(at)
+
+    lax.fori_loop(0, count, inner, 0)
+
+    @pl.when(below)
+    def _():
+        for copy in up:
+            copy.wait_recv()
+        for copy in down:
+            copy.wait_send()
+
+    @pl.when(above)
+    def _():
+        for copy in down:
+            copy.wait_recv()
+        for copy in up:
+            copy.wait_send()
+
+    pe[planes : planes + 2] = pot_near[0, planes - 2 : planes]
+    pe[planes + 2 : planes + 4] = pot_near[1, 0:2]
+    diagonals(slice(planes, planes + 4))
+    for at in (0, 1, planes + 2, planes + 3):
+        spread_plane(at, 0)
+
+    def each_node(node, packed):
+        one_node(node, (0, 1, planes + 2, planes + 3), edge_planes)
 
         @pl.when(jnp.logical_not(below))
         def _():
-            ub[0, 1] = jnp.zeros((cols, cells), jnp.float32)
-            ub[1, 1] = jnp.zeros((cols, cells), jnp.float32)
+            ub[node, 0, 1] = jnp.zeros((cols, cells), jnp.float32)
+            ub[node, 1, 1] = jnp.zeros((cols, cells), jnp.float32)
 
         @pl.when(jnp.logical_not(above))
         def _():
-            ub[0, planes + 2] = jnp.zeros((cols, cells), jnp.float32)
-            ub[1, planes + 2] = jnp.zeros((cols, cells), jnp.float32)
+            ub[node, 0, planes + 2] = jnp.zeros((cols, cells), jnp.float32)
+            ub[node, 1, planes + 2] = jnp.zeros((cols, cells), jnp.float32)
 
         def third(at, sums):
-            u_re, u_im = field(ub, 0, at), field(ub, 1, at)
+            u_re, u_im = field(ub.at[node], 0, at), field(ub.at[node], 1, at)
             for tile in range(reps):
                 s = sext[at, :, lanes(tile)]
                 a_re, a_im = p1[node, 0, at, :, lanes(tile)], p1[node, 1, at, :, lanes(tile)]
@@ -301,8 +322,6 @@
             gath[me, at - 2, :, lanes(tile)] = value
             rhs[at - 2, cols:, lanes(tile)] = value
 
-    for at in range(2, planes + 2):
-        moment(at)
 
     bits = [1 << at for at in range(count.bit_length() - 1)]
     orders = [bits[1:] + bits[:1], bits[1:][::-1] + bits[:1]]
@@ -341,6 +360,20 @@
     edge_up = edge(planes, 0, lax.rem(dom + 1, doms), 0)
     edge_down = edge(1, planes + 1, lax.rem(dom + doms - 1, doms), 1)
 
+    for at in range(2, 2 + half):
+        moment(at)
+    forward(0, 0)
+    for at in range(2 + half, planes + 2):
+        moment(at)
+    forward(0, 1)
+
+    def keep(gap):
+        where = lax.bitwise_xor(me, gap)
+        place = out.at[:, pl.ds(pl.multiple_of(where * cols, 8), cols), :] if sliced else out.at[where]
+        return pltpu.make_async_copy(gath.at[where], place, out_sem.at[gap])
+
+    keep(0).start()
+
     @pl.when(above)
     def _():
         edge_up.start()
@@ -348,9 +381,6 @@
     @pl.when(below)
     def _():
         edge_down.start()
-
-    for part in range(2):
-        forward(0, part)
 
     @pl.when(jnp.logical_not(below))
     def _():
@@ -374,7 +404,7 @@
         get = field(mext, 0, at)
         values = []
         for tile in range(reps):
-            onsite = 6.0 + jnp.broadcast_to(pe[at + 1 : at + 2, lanes(tile)], (cols, LANES))
+            onsite = 6.0 + jnp.broadcast_to(pe[at - 1 : at, lanes(tile)], (cols, LANES))
             values.append(onsite * get(0, tile) - neighbours(get, 0, tile, reps))
         for tile, value in enumerate(gather_back(values)):
             rhs[at - 1, :cols, lanes(tile)] = value
@@ -385,9 +415,13 @@
     arrivals = sorted(
         ((gap, part) for gap in range(1, count) for part in range(2)),
         key=lambda pair: (pair[0] & 1, bin(pair[0]).count("1"), last_of(pair[0], orders[pair[1]]), pair[1]))
+    done = set()
     for gap, part in arrivals:
         arrived(gap, part)
         forward(gap, part)
+        if (gap, 1 - part) in done:
+            keep(gap).start()
+        done.add((gap, part))
 
     def contract(at, value):
         left_hi, left_lo = split(rhs[at])
@@ -405,6 +439,10 @@
     fin[me] = total * (1.0 / total_cells)
     to_all(fin, fin_send, fin_recv, "shift", me, count)
 
+    out_h[...] = fin[:, :cols].reshape(count * cols, count * cols)
+    out_b[...] = fin[:, cols:].reshape(count * cols, count * cols)
+    for gap in range(count):
+        keep(gap).wait()
     for part in range(2):
         for gap in range(count):
             for at in range(last_of(gap, orders[part]) + 1, len(bits)):
@@ -424,23 +462,28 @@
     f32 = jnp.float32
     dma = pltpu.SemaphoreType.DMA
     vmem = pl.BlockSpec(memory_space=pltpu.VMEM)
-    gath, fin = pl.pallas_call(
+    size = count * cols
+    shape = (planes, vectors, cells) if sliced else (count, planes, cols, cells)
+    subspace, reduced_h, reduced_b = pl.pallas_call(
         functools.partial(kernel, count, doms, sliced, planes * doms * cells),
         out_shape=(
-            jax.ShapeDtypeStruct((count, planes, cols, cells), f32),
-            jax.ShapeDtypeStruct((count, 2 * cols, count * cols), f32),
+            jax.ShapeDtypeStruct(shape, f32),
+            jax.ShapeDtypeStruct((size, size), f32),
+            jax.ShapeDtypeStruct((size, size), f32),
         ),
         in_specs=[pl.BlockSpec(memory_space=pl.ANY), vmem],
-        out_specs=(vmem, vmem),
+        out_specs=(pl.BlockSpec(memory_space=pl.ANY), vmem, vmem),
         scratch_shapes=[
+            pltpu.VMEM((count, planes, cols, cells), f32),
+            pltpu.VMEM((count, 2 * cols, size), f32),
             pltpu.VMEM((planes + 4, cols, cells), f32),
             pltpu.VMEM((planes + 4, cols, cells), f32),
             pltpu.VMEM((2, planes, cells), f32),
             pltpu.VMEM((planes + 4, cells), f32),
             pltpu.VMEM((count, 2, planes + 4, cells), f32),
             pltpu.VMEM((count, 2, planes + 4, cells), f32),
-            pltpu.VMEM((2, planes + 4, cols, cells), f32),
-            pltpu.VMEM((2, planes + 4, cols, cells), f32),
+            pltpu.VMEM((count, 2, planes + 4, cols, cells), f32),
+            pltpu.VMEM((count, 2, planes + 4, cols, cells), f32),
             pltpu.VMEM((count, 2, planes + 4, cols, cells), f32),
             pltpu.VMEM((doms, cols, width), f32),
             pltpu.VMEM((count, 4, cols, LANES), f32),
@@ -451,7 +494,7 @@
             dma((2, 2)), dma((2, 2)),
             dma((doms,)), dma((doms,)),
             dma((2,)), dma((2,)),
-            dma((2, count, levels)), dma((2, count)),
+            dma((2, count, levels)), dma((2, count)), dma((count,)),
             dma((doms,)), dma((doms,)),
             dma((count,)), dma((count,)),
         ],
@@ -460,10 +503,14 @@
         ),
         name="feast_step",
     )(samples, potential)
-    subspace = jnp.transpose(gath[:, :, :own], (1, 0, 2, 3)).reshape(planes, vectors, cells)
-    fin = fin.reshape(count, 2, cols, count, cols)[:, :, :own, :, :own]
-    fin = jnp.transpose(fin, (1, 3, 4, 0, 2)).reshape(2, vectors, vectors)
-    return subspace, fin[0], fin[1]
+    if sliced:
+        return subspace, reduced_h, reduced_b
+    subspace = jnp.transpose(subspace[:, :, :own], (1, 0, 2, 3)).reshape(planes, vectors, cells)
+
+    def trim(value):
+        return value.reshape(count, cols, count, cols)[:, :own, :, :own].reshape(vectors, vectors)
+
+    return subspace, trim(reduced_h), trim(reduced_b)
 
 
 def solution(mesh):

time: 55.9 us -> 51 us (0.912)
  Pallas kernels: 50 us -> 45.7 us
  local copies, waits for them, and re-layouts: 5.06 us -> 4.41 us
    unnamed x2 -> x7, local copies, waits for them, and re-layouts: 0.01 us -> 4.41 us
    pallas_call x1, Pallas kernels: 50 us -> 45.7 us  [on_device(): pl.pallas_call(functools.partial(kernel, count, doms, sliced, planes * do...]
    reshape x2 -> x0, local copies, waits for them, and re-layouts: 3.37 us -> none  [the longest x1 3.19 us: on_device(): jnp.transpose(gath[:, :, :own], (1, 0, 2, 3))]
    squeeze x4 -> x0, local copies, waits for them, and re-layouts: 1.65 us -> none  [on_device(): return (subspace, fin[0], fin[1])]
where the time goes in v3:
time: 51 us; the launch traced here: 50.8 us
  Pallas kernels  45.7 us (90%)
  local copies, waits for them, and re-layouts  4.41 us (9%)
  between operations  0.66 us (1%)
    pallas_call x1, Pallas kernels, on_device(): pl.pallas_call(functools.partial(kernel, count, doms, sliced, planes * do...  45.7 us
    unnamed x7, local copies, waits for them, and re-layouts  4.41 us

profile of v3, /device:TPU:0, one launch (start us, length us, event | category | flops | bytes accessed | tf_op | source)
XLA Modules:
  0.0 50.8 jit_solution(3774542150798885927)
XLA Ops:
  0.6 45.7 %feast_step.1 = (f32[8,64,1024]{2,1,0:T(8,128)}, f32[64,64]{1,0:T(8,128)}, f32[64,64]{1,0:T(8,128)}) custom-call(f32[8,64,1024]{2,1,0:T(8,128)} %samples.1, f32[8,1024]{1,0:T(8,128)} %pot.1), custom_call_target="tpu_custom_call" | custom-call | tf_op jit(solution)/shard_map/feast_step/pallas_call | solution.py:467
  46.3 0.0 copy-start.1
  46.3 0.0 copy-start
  46.3 3.2 %copy.8 = f32[8,64,1024]{2,1,0:T(8,128)} copy(f32[8,64,1024]{2,1,0:T(8,128)} %get-tuple-element.6) | data formatting | bytes 4194304
  49.5 0.0 copy-done.1
  49.5 0.6 %copy.9 = f32[64,64]{1,0:T(8,128)} copy(f32[64,64]{1,0:T(8,128)S(1)} %copy-done.1) | data formatting | bytes 32768
  50.1 0.0 copy-done
  50.1 0.6 %copy.10 = f32[64,64]{1,0:T(8,128)} copy(f32[64,64]{1,0:T(8,128)S(1)} %copy-done) | data formatting | bytes 32768
Async XLA Ops:
  46.3 3.2 %copy-start.1 = (f32[64,64]{1,0:T(8,128)S(1)}, f32[64,64]{1,0:T(8,128)}, u32[]{:S(2)}) copy-start(f32[64,64]{1,0:T(8,128)} %get-tuple-element.7) | copy-start | bytes 49156
  46.3 3.8 %copy-start = (f32[64,64]{1,0:T(8,128)S(1)}, f32[64,64]{1,0:T(8,128)}, u32[]{:S(2)}) copy-start(f32[64,64]{1,0:T(8,128)} %get-tuple-element.8) | copy-start | bytes 49156

commit v4 on v3

--- a/solution.py
+++ b/solution.py
@@ -462,6 +462,9 @@
     f32 = jnp.float32
     dma = pltpu.SemaphoreType.DMA
     vmem = pl.BlockSpec(memory_space=pltpu.VMEM)
+    plane = cols * cells * 4
+    held = 6 * count * (planes + 4) * plane + 4 * count * (planes + 16) * cells * 4
+    held += (count + 10) * (planes + 4) * plane
     size = count * cols
     shape = (planes, vectors, cells) if sliced else (count, planes, cols, cells)
     subspace, reduced_h, reduced_b = pl.pallas_call(
@@ -471,7 +474,7 @@
             jax.ShapeDtypeStruct((size, size), f32),
             jax.ShapeDtypeStruct((size, size), f32),
         ),
-        in_specs=[pl.BlockSpec(memory_space=pl.ANY), vmem],
+        in_specs=[pl.BlockSpec(memory_space=pltpu.HBM), vmem],
         out_specs=(pl.BlockSpec(memory_space=pl.ANY), vmem, vmem),
         scratch_shapes=[
             pltpu.VMEM((count, planes, cols, cells), f32),
@@ -499,7 +502,7 @@
             dma((count,)), dma((count,)),
         ],
         compiler_params=pltpu.CompilerParams(
-            collective_id=0, has_side_effects=True, vmem_limit_bytes=56 * 1024 * 1024
+            collective_id=0, has_side_effects=True, vmem_limit_bytes=min(held + 2 * 1024 * 1024, 60 * 1024 * 1024)
         ),
         name="feast_step",
     )(samples, potential)

time: 51 us -> 49.9 us (0.978)
  Pallas kernels: 45.7 us -> 44.2 us
    pallas_call x1, Pallas kernels: 45.7 us -> 44.2 us  [on_device(): pl.pallas_call(functools.partial(kernel, count, doms, sliced, planes * do...]
where the time goes in v4:
time: 49.9 us; the launch traced here: 49.7 us
  Pallas kernels  44.2 us (89%)
  local copies, waits for them, and re-layouts  4.89 us (10%)
  between operations  0.65 us (1%)
    pallas_call x1, Pallas kernels, on_device(): pl.pallas_call(functools.partial(kernel, count, doms, sliced, planes * do...  44.2 us
    unnamed x7, local copies, waits for them, and re-layouts  4.89 us

profile of v4, /device:TPU:0, one launch (start us, length us, event | category | flops | bytes accessed | tf_op | source)
XLA Modules:
  0.0 49.7 jit_solution(18280555556611999225)
XLA Ops:
  0.6 0.0 copy-start
  0.6 1.6 %copy-done = f32[8,64,1024]{2,1,0:T(8,128)S(1)} copy-done((f32[8,64,1024]{2,1,0:T(8,128)S(1)}, f32[8,64,1024]{2,1,0:T(8,128)}, u32[]{:S(2)}) %copy-start) | copy-done | bytes 2097176
  2.2 0.0 copy-start.1
  2.2 0.8 %copy-done.1 = f32[8,1024]{1,0:T(8,128)S(1)} copy-done((f32[8,1024]{1,0:T(8,128)S(1)}, f32[8,1024]{1,0:T(8,128)}, u32[]{:S(2)}) %copy-start.1) | copy-done | bytes 32792
  3.0 44.2 %feast_step.1 = (f32[8,64,1024]{2,1,0:T(8,128)S(1)}, f32[64,64]{1,0:T(8,128)S(1)}, f32[64,64]{1,0:T(8,128)S(1)}) custom-call(f32[8,64,1024]{2,1,0:T(8,128)S(1)} %copy-done, f32[8,1024]{1,0:T(8,128)S(1)} %copy-done.1), custom_call_target="tpu_custom_call" | custom-call | tf_op jit(solution)/shard_map/feast_step/pallas_call | solution.py:470
  47.2 1.3 %copy.8 = f32[8,64,1024]{2,1,0:T(8,128)} copy(f32[8,64,1024]{2,1,0:T(8,128)S(1)} %get-tuple-element.6) | data formatting | bytes 4194304
  48.5 0.6 %copy.9 = f32[64,64]{1,0:T(8,128)} copy(f32[64,64]{1,0:T(8,128)S(1)} %get-tuple-element.7) | data formatting | bytes 32768
  49.1 0.6 %copy.10 = f32[64,64]{1,0:T(8,128)} copy(f32[64,64]{1,0:T(8,128)S(1)} %get-tuple-element.8) | data formatting | bytes 32768
Async XLA Ops:
  0.6 1.6 %copy-start = (f32[8,64,1024]{2,1,0:T(8,128)S(1)}, f32[8,64,1024]{2,1,0:T(8,128)}, u32[]{:S(2)}) copy-start(f32[8,64,1024]{2,1,0:T(8,128)} %samples.1) | copy-start | bytes 6291460
  2.2 0.8 %copy-start.1 = (f32[8,1024]{1,0:T(8,128)S(1)}, f32[8,1024]{1,0:T(8,128)}, u32[]{:S(2)}) copy-start(f32[8,1024]{1,0:T(8,128)} %pot.1) | copy-start | bytes 98308
